TPU v7x, 128 devices: a whole 4x4x4 slice. The times are simulated.
128 devices in a mesh: row: 16 (over x, z), col: 8 (over y, core).
Axes of the slice: x: 4, y: 4, z: 4, core: 2. Of those that a mesh axis runs over, the one named last changes fastest.
Arguments:
- front: float32 [9216, 9216], P('row', 'col')
- child_tiles: float32 [16384, 4096], P(('row', 'col')), may hold values from -0.4375 to 0.4375
- tile_target: int32 [16384], P(('row', 'col')), may hold values from 0 to 20735, as said below
- tile_count: int32 [512], P(('row', 'col')), may hold values from 24 to 32
- probe: float32 [9216, 512], P('col'), may hold values from -1.75 to 1.75
Outputs:
- panel_factor: float32 [9216, 1024], P('row', 'col')
- sketch: float32 [9216, 512], P('row', 'col')
Inputs may be any that keep to these rules, and one draw needn't show every extreme that they name: `tile_target`: among the 128 slots of one device, live or not, each counted once at its target tile and once at the mirrored tile, at most 2 placements fall inside the block of the front held by any one device.
All inputs are finite; a program needn't handle non-finite values.
Results may differ from a plain program's by a relative error of at most 0.00015.
Values sent between devices are 32-bit elements; how exact they have to be, the bound alone decides.
A program may use at most 128 MiB of HBM per device.

v0:
```python
import jax
import jax.numpy as jnp
from jax import lax
from jax.sharding import PartitionSpec as P

NB = 512
PANELS = 2
TB = 64
SLOTS = 32
HIGH = lax.Precision.HIGHEST


def in_blocks(value, dim, size):
    before, after = (value.shape[:dim], value.shape[dim + 1 :])
    return jnp.moveaxis(value.reshape(*before, size, -1, *after), dim, 0)


def joined_along(tiles, dim):
    lengths = list(tiles.shape[1:])
    lengths[dim] *= tiles.shape[0]
    return jnp.moveaxis(tiles, 0, dim).reshape(lengths)


def one_exchange(value, axis, axes, splits, concats):
    sizes = [lax.axis_size(a) for a in axes]
    tiles = in_blocks(value, splits[0], sizes[0])
    tiles = jnp.moveaxis(in_blocks(tiles, splits[1] + 1, sizes[1]), 0, 1)
    inside = tiles.shape[2:]
    tiles = tiles.reshape(-1, *inside)
    tiles = lax.all_to_all(tiles, axis, split_axis=0, concat_axis=0, tiled=True)
    tiles = joined_along(tiles.reshape(*sizes, *inside), concats[0] + 1)
    return joined_along(tiles, concats[1])


def filled_up(lines, size):
    spare = -lines.shape[0] % size
    if not spare:
        return lines
    return jnp.concatenate([lines, jnp.zeros((spare, *lines.shape[1:]), lines.dtype)])


def from_root(value, axis, root):
    lines = jnp.where(lax.axis_index(axis) == root, value, jnp.zeros_like(value)).reshape(
        -1, *value.shape[1:][-1:]
    )
    padded = filled_up(lines, lax.axis_size(axis))
    own = lax.psum_scatter(padded, axis, scatter_dimension=0, tiled=True)
    return lax.all_gather(own, axis, axis=0, tiled=True)[: len(lines)].reshape(value.shape)


def broadcast(value, axis, root):
    mine = lax.axis_index(axis) == root
    return lax.psum(jnp.where(mine, value, jnp.zeros_like(value)), axis)


def sum_at_owner(value, axis, dim):
    tiles = in_blocks(value, dim, lax.axis_size(axis))
    arrived = lax.all_to_all(tiles, axis, split_axis=0, concat_axis=0, tiled=True)
    return arrived.sum(axis=0)


def per_device(front, child_tiles, tile_target, tile_count, probe):
    row_count = lax.axis_size("row")
    col_count = lax.axis_size("col")
    devices = row_count * col_count
    local_rows, local_cols = front.shape
    tile_rows = local_rows // TB
    tile_cols = local_cols // TB
    grid = tile_cols * col_count
    local_tiles = tile_rows * tile_cols
    held = child_tiles.shape[0]
    capacity = 2 * max(1, (held + devices - 1) // devices)
    slot_index = jnp.arange(held, dtype=jnp.int32)
    live_once = slot_index % SLOTS < tile_count[slot_index // SLOTS]
    live = jnp.concatenate([live_once, live_once])
    mirrored = child_tiles.reshape(held, TB, TB).transpose(0, 2, 1).reshape(held, TB * TB)
    placements = jnp.concatenate([child_tiles, mirrored], axis=0)
    first_row = tile_target // grid
    first_col = tile_target % grid
    target_row = jnp.concatenate([first_row, first_col])
    target_col = jnp.concatenate([first_col, first_row])
    owner = target_row // tile_rows * col_count + target_col // tile_cols
    place = target_row % tile_rows * tile_cols + target_col % tile_cols
    onehot = (
        (owner[:, None] == jnp.arange(devices, dtype=jnp.int32)[None, :]) & live[:, None]
    ).astype(jnp.int32)
    earlier = jnp.cumsum(onehot, axis=0) - onehot
    rank = jnp.sum(earlier * onehot, axis=1)
    slot = jnp.where(live, owner * capacity + rank, devices * capacity)
    outgoing = (
        jnp.zeros((devices * capacity + 1, TB * TB), jnp.float32).at[slot].set(placements)[:-1]
    )
    where_to = jnp.full((devices * capacity + 1,), local_tiles, jnp.int32).at[slot].set(place)[:-1]
    shaped = (
        outgoing.reshape(row_count, col_count * capacity, TB * TB),
        where_to.reshape(row_count, col_count * capacity),
    )
    incoming, landing = (
        one_exchange(shaped[0], ("row", "col"), ("row", "col"), (0, 1), (0, 1)),
        one_exchange(shaped[1], ("row", "col"), ("row", "col"), (0, 1), (0, 1)),
    )
    incoming = incoming.reshape(-1, TB * TB)
    landing = landing.reshape(-1)
    extend = (
        jnp.zeros((local_tiles + 1, TB * TB), jnp.float32).at[landing].add(incoming)[:local_tiles]
    )
    extend = (
        extend.reshape(tile_rows, tile_cols, TB, TB)
        .transpose(0, 2, 1, 3)
        .reshape(local_rows, local_cols)
    )
    matrix = front + extend
    row_start = lax.axis_index("row") * local_rows
    col_start = lax.axis_index("col") * local_cols
    global_rows = row_start + jnp.arange(local_rows, dtype=jnp.int32)
    group = row_count // col_count
    margin = jnp.zeros((NB, NB), jnp.float32)
    factor_parts = []
    for k in range(PANELS):
        low = k * NB
        high = low + NB
        owner_col = low // local_cols
        offset = low % local_cols
        panel = from_root(matrix[:, offset : offset + NB], "col", owner_col)
        padded = jnp.concatenate([margin, panel, margin], axis=0)
        begin = jnp.clip(low - row_start + NB, 0, local_rows + NB)
        piece = lax.dynamic_slice_in_dim(padded, begin, NB, 0)
        diag_block = lax.psum(piece, "row")
        chol = jnp.linalg.cholesky(0.5 * (diag_block + diag_block.T))
        solved = jax.scipy.linalg.solve_triangular(chol, panel.T, lower=True).T
        factor_parts.append(jnp.where((global_rows >= low)[:, None], solved, 0.0))
        trail = jnp.where((global_rows >= high)[:, None], solved, 0.0)
        column_owner = lax.axis_index("col") * group
        pieces = [broadcast(trail, "row", column_owner + member) for member in range(group)]
        across = jnp.concatenate(pieces, axis=0)
        matrix = matrix - jnp.dot(trail, across.T, precision=HIGH)
    start = PANELS * NB
    global_cols = col_start + jnp.arange(local_cols, dtype=jnp.int32)
    weighted = jnp.where((global_cols >= start)[:, None], probe, 0.0)
    shares = sum_at_owner(
        lax.dot_general(weighted, matrix, (((0,), (1,)), ((), ())), precision=HIGH), "col", 0
    )
    sketch = jnp.where((global_rows >= start)[:, None], shares.T, 0.0)
    all_panels = jnp.concatenate(factor_parts, axis=1)
    width = all_panels.shape[1] // col_count
    panel_factor = lax.dynamic_slice_in_dim(all_panels, lax.axis_index("col") * width, width, 1)
    return (panel_factor, sketch)


def solution(mesh):
    return jax.shard_map(
        per_device,
        mesh=mesh,
        in_specs=(
            P("row", "col"),
            P(("row", "col"), None),
            P(("row", "col")),
            P(("row", "col")),
            P("col", None),
        ),
        out_specs=(P("row", "col"), P("row", "col")),
        check_vma=False,
    )
```

profile of v0, /device:TPU:1, one launch (start us, length us, event | category | flops | bytes accessed | tf_op | source)
XLA Modules:
  0.0 1003.4 jit_solution(17757820655012956910)
XLA Ops:
  17.6 11.5 %all-to-all-start = ((s32[128,1,2]{2,1,0:T(1,128)}), s32[128,1,2]{2,1,0:T(1,128)S(1)}, u32[]{:S(2)}, u32[]{:S(2)}) async-start(s32[128,1,2]{2,1,0:T(1,128)} %bitcast.16), calls=%async_computation | async-start | bytes 131072 | tf_op jit(solution)/shard_map/all_to_all | solution.py:30
  57.4 10.2 %all-to-all-start.1 = ((f32[128,1,2,4096]{3,2,1,0:T(2,128)}), f32[128,1,2,4096]{3,2,1,0:T(2,128)}, u32[]{:S(2)}, u32[]{:S(2)}) async-start(f32[128,1,2,4096]{3,2,1,0:T(2,128)} %bitcast.188), calls=%async_computation.1 | async-start | bytes 8388608 | tf_op jit(solution)/shard_map/all_to_all | solution.py:30
  68.0 52.1 %all-to-all-done.1 = f32[128,1,2,4096]{3,2,1,0:T(2,128)} async-done(((f32[128,1,2,4096]{3,2,1,0:T(2,128)}), f32[128,1,2,4096]{3,2,1,0:T(2,128)}, u32[]{:S(2)}, u32[]{:S(2)}) %all-to-all-start.1) | async-done | bytes 4194336 | tf_op jit(solution)/shard_map/all_to_all | solution.py:30
  126.1 8.4 scatter_custom_fusion.2
  138.9 8.6 copy.37
  157.8 27.1 %reduce-scatter.3.cloned.1.call-done = f32[72,512]{1,0:T(8,128)} async-done(((f32[576,512]{1,0:T(8,128)}), f32[72,512]{1,0:T(8,128)}) %reduce-scatter.3.cloned.1.call-update) | async-done | bytes 147472 | tf_op jit(solution)/shard_map/reduce_scatter | solution.py:47
  184.9 27.1 %all-gather.3.cloned.1.call-done = f32[576,512]{1,0:T(8,128)} async-done(((f32[72,512]{1,0:T(8,128)}), f32[576,512]{1,0:T(8,128)}) %all-gather.3.cloned.1.call-update) | async-done | bytes 1179664 | tf_op jit(solution)/shard_map/all_gather | solution.py:48
  216.5 84.9 %all-reduce.8.cloned.1.call-done = f32[512,512]{1,0:T(8,128)} async-done(((f32[512,512]{1,0:T(8,128)}), f32[512,512]{1,0:T(8,128)}) %all-reduce.8.cloned.1.call-update) | async-done | bytes 1048592 | tf_op jit(solution)/shard_map/psum | solution.py:128
  312.1 11.7 %cholesky.286 = f32[128,128]{1,0:T(8,128)S(1)} custom-call(f32[128,128]{1,0:T(8,128)S(1)} %cholesky.426), custom_call_target="Cholesky" | custom-call | tf_op jit(solution)/shard_map/jit(cholesky)/cholesky | solution.py:129
  325.0 9.8 custom-call.27
  338.0 11.7 %cholesky.305 = f32[128,128]{1,0:T(8,128)S(1)} custom-call(f32[128,128]{1,0:T(8,128)S(1)} %cholesky.430), custom_call_target="Cholesky" | custom-call | tf_op jit(solution)/shard_map/jit(cholesky)/cholesky | solution.py:129
  350.4 10.0 custom-call.28
  362.7 11.7 %cholesky.326 = f32[128,128]{1,0:T(8,128)S(1)} custom-call(f32[128,128]{1,0:T(8,128)S(1)} %cholesky.435), custom_call_target="Cholesky" | custom-call | tf_op jit(solution)/shard_map/jit(cholesky)/cholesky | solution.py:129
  375.7 9.8 custom-call.29
  387.8 12.1 %cholesky.343 = f32[128,128]{1,0:T(8,128)S(1)} custom-call(f32[128,128]{1,0:T(8,128)S(1)} %convolution_subtract_fusion.13), custom_call_target="Cholesky" | custom-call | tf_op jit(solution)/shard_map/jit(cholesky)/cholesky | solution.py:129
  406.8 11.9 %while.4 = (s32[]{:T(128)}, f32[512,512]{1,0:T(8,128)}, s32[4,2]{0,1:T(2,128)S(1)}, f32[4,128,128]{2,1,0:T(8,128)S(1)}, s32[]{:T(128)}) while((s32[]{:T(128)}, f32[512,512]{1,0:T(8,128)}, s32[4,2]{0,1:T(2,128)S(1)}, f32[4,128,128]{2,1,0:T(8,128)S(1)}, s32[]{:T(128)}) %tuple.68), condition=%wide.while_cond, body=%wide.while_body.sunk | while | flops 2 | bytes 131181 | solution.py:130
  418.8 39.3 %custom-call.30 = f32[4,128,128]{1,2,0:T(8,128)S(1)} custom-call(f32[4,128,128]{2,1,0:T(8,128)S(1)} %get-tuple-element.18), custom_call_target="InvertDiagBlocksLowerTriangular" | custom-call | tf_op jit(solution)/shard_map/jit(_solve_triangular)/triangular_solve | solution.py:130
  469.5 91.7 %all-reduce.14.cloned.1.call-done = (f32[576,512]{1,0:T(8,128)}, f32[576,512]{1,0:T(8,128)}) async-done(((f32[576,512]{1,0:T(8,128)}, f32[576,512]{1,0:T(8,128)}), (f32[576,512]{1,0:T(8,128)}, f32[576,512]{1,0:T(8,128)})) %all-reduce.14.cloned.1.call-update) | async-done | bytes 2359312 | tf_op jit(solution)/shard_map/psum | solution.py:53
  570.8 30.4 %reduce-scatter.5.cloned.1.call-done = f32[72,512]{1,0:T(8,128)} async-done(((f32[576,512]{1,0:T(8,128)}), f32[72,512]{1,0:T(8,128)}) %reduce-scatter.5.cloned.1.call-update) | async-done | bytes 147472 | tf_op jit(solution)/shard_map/reduce_scatter | solution.py:47
  601.3 26.9 %all-gather.5.cloned.1.call-done = f32[576,512]{1,0:T(8,128)} async-done(((f32[72,512]{1,0:T(8,128)}), f32[576,512]{1,0:T(8,128)}) %all-gather.5.cloned.1.call-update) | async-done | bytes 1179664 | tf_op jit(solution)/shard_map/all_gather | solution.py:48
  631.0 86.2 %all-reduce.10.cloned.1.call-done = f32[512,512]{1,0:T(8,128)} async-done(((f32[512,512]{1,0:T(8,128)}), f32[512,512]{1,0:T(8,128)}) %all-reduce.10.cloned.1.call-update) | async-done | bytes 1048592 | tf_op jit(solution)/shard_map/psum | solution.py:128
  720.1 11.7 %cholesky.358 = f32[128,128]{1,0:T(8,128)S(1)} custom-call(f32[128,128]{1,0:T(8,128)S(1)} %cholesky.439), custom_call_target="Cholesky" | custom-call | tf_op jit(solution)/shard_map/jit(cholesky)/cholesky | solution.py:129
  732.0 9.8 custom-call.31
  742.5 11.7 %cholesky.377 = f32[128,128]{1,0:T(8,128)S(1)} custom-call(f32[128,128]{1,0:T(8,128)S(1)} %cholesky.443), custom_call_target="Cholesky" | custom-call | tf_op jit(solution)/shard_map/jit(cholesky)/cholesky | solution.py:129
  755.5 10.2 %custom-call.32 = f32[1,128,128]{1,2,0:T(8,128)S(1)} custom-call(f32[1,128,128]{2,1,0:T(8,128)S(1)} %get-tuple-element.58), custom_call_target="InvertDiagBlocksLowerTriangular" | custom-call | tf_op jit(solution)/shard_map/jit(cholesky)/cholesky | solution.py:129
  766.4 11.7 %cholesky.398 = f32[128,128]{1,0:T(8,128)S(1)} custom-call(f32[128,128]{1,0:T(8,128)S(1)} %cholesky.448), custom_call_target="Cholesky" | custom-call | tf_op jit(solution)/shard_map/jit(cholesky)/cholesky | solution.py:129
  778.7 9.8 custom-call.33
  789.2 11.9 %cholesky.415 = f32[128,128]{1,0:T(8,128)S(1)} custom-call(f32[128,128]{1,0:T(8,128)S(1)} %convolution_subtract_fusion.12), custom_call_target="Cholesky" | custom-call | tf_op jit(solution)/shard_map/jit(cholesky)/cholesky | solution.py:129
  812.1 39.3 %custom-call.34 = f32[4,128,128]{1,2,0:T(8,128)S(1)} custom-call(f32[4,128,128]{2,1,0:T(8,128)S(1)} %get-tuple-element.19), custom_call_target="InvertDiagBlocksLowerTriangular" | custom-call | tf_op jit(solution)/shard_map/jit(_solve_triangular)/triangular_solve | solution.py:130
  859.8 91.7 %all-reduce.12.cloned.1.call-done = (f32[576,512]{1,0:T(8,128)}, f32[576,512]{1,0:T(8,128)}) async-done(((f32[576,512]{1,0:T(8,128)}, f32[576,512]{1,0:T(8,128)}), (f32[576,512]{1,0:T(8,128)}, f32[576,512]{1,0:T(8,128)})) %all-reduce.12.cloned.1.call-update) | async-done | bytes 2359312 | tf_op jit(solution)/shard_map/psum | solution.py:53
  958.6 12.7 %fusion.6 = f32[512,576]{1,0:T(8,128)} fusion(f32[576,1152]{1,0:T(8,128)S(1)} %convolution_subtract_fusion, f32[1152,512]{1,0:T(8,128)S(1)} %copy-done.12, pred[1152]{0:T(1024)(128)(4,1)S(1)} %add_compare_fusion), kind=kOutput, calls=%fused_computation.24 | convolution fusion | flops 4077453312 | bytes 6194304 | tf_op jit(solution)/shard_map/dot_general | solution.py:141
  978.6 17.0 %all-to-all-done.2 = f32[8,64,576]{2,1,0:T(8,128)S(1)} async-done(((f32[8,64,576]{2,1,0:T(8,128)}), f32[8,64,576]{2,1,0:T(8,128)S(1)}, u32[]{:S(2)}, u32[]{:S(2)}) %all-to-all-start.2) | async-done | bytes 1179680 | tf_op jit(solution)/shard_map/all_to_all | solution.py:58
  (187 shorter events, 172.3 us)
Async XLA Ops:
  17.6 39.7 %all-to-all-start = ((s32[128,1,2]{2,1,0:T(1,128)}), s32[128,1,2]{2,1,0:T(1,128)S(1)}, u32[]{:S(2)}, u32[]{:S(2)}) async-start(s32[128,1,2]{2,1,0:T(1,128)} %bitcast.16), calls=%async_computation | async-start | bytes 131072 | tf_op jit(solution)/shard_map/all_to_all | solution.py:30
  57.4 62.7 %all-to-all-start.1 = ((f32[128,1,2,4096]{3,2,1,0:T(2,128)}), f32[128,1,2,4096]{3,2,1,0:T(2,128)}, u32[]{:S(2)}, u32[]{:S(2)}) async-start(f32[128,1,2,4096]{3,2,1,0:T(2,128)} %bitcast.188), calls=%async_computation.1 | async-start | bytes 8388608 | tf_op jit(solution)/shard_map/all_to_all | solution.py:30
  67.6 117.3 %reduce-scatter.3.cloned.1.call-start = ((), (), s32[]{:S(2)}) async-start(), calls=%async_computation.5 | async-start | bytes 1327104 | tf_op jit(solution)/shard_map/reduce_scatter | solution.py:47
  157.7 54.3 %all-gather.3.cloned.1.call-start = ((), (), s32[]{:S(2)}) async-start(), calls=%async_computation.6 | async-start | bytes 1327104 | tf_op jit(solution)/shard_map/all_gather | solution.py:48
  184.9 116.6 %all-reduce.8.cloned.1.call-start = ((), (), s32[]{:S(2)}) async-start(), calls=%async_computation.7 | async-start | bytes 2097152 | tf_op jit(solution)/shard_map/psum | solution.py:128
  212.1 1.0 copy-start.2
  216.0 345.1 %all-reduce.14.cloned.1.call-start = ((), (), s32[]{:S(2)}) async-start(), calls=%async_computation.12 | async-start | bytes 4718592 | tf_op jit(solution)/shard_map/psum | solution.py:53
  311.1 1.0 copy-start.9
  458.1 3.3 copy-start.13
  458.1 3.3 copy-start.4
  467.3 2.1 copy-start.11
  469.4 131.8 %reduce-scatter.5.cloned.1.call-start = ((), (), s32[]{:S(2)}) async-start(), calls=%async_computation.8 | async-start | bytes 1327104 | tf_op jit(solution)/shard_map/reduce_scatter | solution.py:47
  568.0 1.5 copy-start
  570.7 57.5 %copy-start.3 = (f32[512,512]{1,0:T(8,128)S(1)}, f32[512,512]{1,0:T(8,128)}, u32[]{:S(2)}) copy-start(f32[512,512]{1,0:T(8,128)} %copy-done.2) | copy-start | bytes 3145732
  570.8 57.4 %all-gather.5.cloned.1.call-start = ((), (), s32[]{:S(2)}) async-start(), calls=%async_computation.9 | async-start | bytes 1327104 | tf_op jit(solution)/shard_map/all_gather | solution.py:48
  601.3 116.0 %all-reduce.10.cloned.1.call-start = ((), (), s32[]{:S(2)}) async-start(), calls=%async_computation.10 | async-start | bytes 2097152 | tf_op jit(solution)/shard_map/psum | solution.py:128
  630.8 320.8 %all-reduce.12.cloned.1.call-start = ((), (), s32[]{:S(2)}) async-start(), calls=%async_computation.11 | async-start | bytes 4718592 | tf_op jit(solution)/shard_map/psum | solution.py:53
  717.2 1.7 copy-start.7
  804.3 47.2 %copy-start.5 = (f32[576,512]{1,0:T(8,128)S(1)}, f32[576,512]{1,0:T(8,128)}, u32[]{:S(2)}) copy-start(f32[576,512]{1,0:T(8,128)} %all-gather.5.cloned.1.call-done) | copy-start | bytes 3538948
  812.1 39.3 %copy-start.8 = (f32[512,512]{1,0:T(8,128)}, f32[512,512]{1,0:T(8,128)S(1)}, u32[]{:S(2)}) copy-start(f32[512,512]{1,0:T(8,128)S(1)} %get-tuple-element.216) | copy-start | bytes 3145732
  857.6 2.1 copy-start.10
  857.7 93.9 %copy-start.1 = (f32[576,1152]{1,0:T(8,128)S(1)}, f32[576,1152]{1,0:T(8,128)}, u32[]{:S(2)}) copy-start(f32[576,1152]{1,0:T(8,128)} %copy-done) | copy-start | bytes 7962628
  951.6 7.0 copy-start.12
  971.3 6.5 copy-start.6
  971.3 24.3 %all-to-all-start.2 = ((f32[8,64,576]{2,1,0:T(8,128)}), f32[8,64,576]{2,1,0:T(8,128)S(1)}, u32[]{:S(2)}, u32[]{:S(2)}) async-start(f32[8,64,576]{2,1,0:T(8,128)} %bitcast.63), calls=%async_computation.4 | async-start | bytes 2621440 | tf_op jit(solution)/shard_map/all_to_all | solution.py:58
Sparse Core Ops, SparseCore 0:
  157.8 26.9 reduce-scatter.2
  186.5 25.4 all-gather.2
  216.2 85.2 all-reduce.7
  469.5 91.5 all-reduce.13
  570.9 30.2 reduce-scatter.4
  602.8 25.3 all-gather.4
  631.4 85.7 all-reduce.9
  859.9 91.6 all-reduce.11
where the time goes:
time: 1010 us; the launch traced here: 1000 us
  waiting for transfers between devices  535 us (53%)
  other arithmetic  280 us (28%)
  local copies, waits for them, and re-layouts  87.2 us (9%)
  matrix products  51.5 us (5%)
  starting transfers between devices  29.3 us (3%)
  between operations  20 us (2%)
    psum x2, waiting for transfers between devices, broadcast(): return lax.psum(jnp.where(mine, value, jnp.zeros_like(value)), axis)  183 us
    psum x2, waiting for transfers between devices, per_device(): diag_block = lax.psum(piece, 'row')  171 us
    another operation x29, other arithmetic, per_device(): chol = jnp.linalg.cholesky(0.5 * (diag_block + diag_block.T))  160 us
    another operation x5, other arithmetic, per_device(): solved = jax.scipy.linalg.solve_triangular(chol, panel.T, lower=True).T  81.2 us
    reduce_scatter x2, waiting for transfers between devices, from_root(): own = lax.psum_scatter(padded, axis, scatter_dimension=0, tiled=True)  57.5 us
    all_gather x2, waiting for transfers between devices, from_root(): lax.all_gather(own, axis, axis=0, tiled=True)[:len(lines)]  53.9 us
    all_to_all x2, waiting for transfers between devices, one_exchange(): tiles = lax.all_to_all(tiles, axis, split_axis=0, concat_axis=0, tiled=True)  52.1 us
    all_to_all x2, starting transfers between devices, one_exchange(): tiles = lax.all_to_all(tiles, axis, split_axis=0, concat_axis=0, tiled=True)  21.7 us
  transfers between devices with their start and end apart: 11, of which 10 were waited for; matrix products, arithmetic and copies ran while one was open for 3% of the time, Pallas kernels for 0%

commit v1 on v0

--- a/solution.py
+++ b/solution.py
@@ -8,6 +8,14 @@
 TB = 64
 SLOTS = 32
 HIGH = lax.Precision.HIGHEST
+
+
+def added_up(array, axis):
+    size, acc = (lax.axis_size(axis), array)
+    for far in [1 << k for k in range(size.bit_length() - 1)]:
+        pairs = [(i, i ^ far) for i in range(size)]
+        acc = acc + lax.ppermute(acc, axis, pairs)
+    return acc
 
 
 def in_blocks(value, dim, size):
@@ -125,7 +133,7 @@
         padded = jnp.concatenate([margin, panel, margin], axis=0)
         begin = jnp.clip(low - row_start + NB, 0, local_rows + NB)
         piece = lax.dynamic_slice_in_dim(padded, begin, NB, 0)
-        diag_block = lax.psum(piece, "row")
+        diag_block = added_up(piece, "row")
         chol = jnp.linalg.cholesky(0.5 * (diag_block + diag_block.T))
         solved = jax.scipy.linalg.solve_triangular(chol, panel.T, lower=True).T
         factor_parts.append(jnp.where((global_rows >= low)[:, None], solved, 0.0))

time: 1010 us -> 1050 us (1.040)
  starting transfers between devices: 29.3 us -> 42.7 us
  waiting for transfers between devices: 535 us -> 547 us
    ppermute x0 -> x8, waiting for transfers between devices: none -> 179 us  [added_up(): acc = acc + lax.ppermute(acc, axis, pairs)]
    psum x2 -> x0, waiting for transfers between devices: 171 us -> none  [per_device(): diag_block = lax.psum(piece, 'row')]
    ppermute x0 -> x8, starting transfers between devices: none -> 14 us  [added_up(): acc = acc + lax.ppermute(acc, axis, pairs)]
  transfers between devices with their start and end apart: 11 -> 17, of which waited for: 10 -> 16; matrix products, arithmetic and copies ran while one was open for 3% -> 3% of each run, Pallas kernels for 0% -> 0%
where the time goes in v1:
time: 1050 us; the launch traced here: 1040 us
  waiting for transfers between devices  547 us (52%)
  other arithmetic  289 us (28%)
  local copies, waits for them, and re-layouts  88.9 us (8%)
  matrix products  50.2 us (5%)
  starting transfers between devices  42.7 us (4%)
  between operations  20.3 us (2%)
    psum x2, waiting for transfers between devices, broadcast(): return lax.psum(jnp.where(mine, value, jnp.zeros_like(value)), axis)  187 us
    ppermute x8, waiting for transfers between devices, added_up(): acc = acc + lax.ppermute(acc, axis, pairs)  179 us
    another operation x29, other arithmetic, per_device(): chol = jnp.linalg.cholesky(0.5 * (diag_block + diag_block.T))  162 us
    another operation x5, other arithmetic, per_device(): solved = jax.scipy.linalg.solve_triangular(chol, panel.T, lower=True).T  81.1 us
    reduce_scatter x2, waiting for transfers between devices, from_root(): own = lax.psum_scatter(padded, axis, scatter_dimension=0, tiled=True)  57.5 us
    all_gather x2, waiting for transfers between devices, from_root(): lax.all_gather(own, axis, axis=0, tiled=True)[:len(lines)]  54 us
    all_to_all x2, waiting for transfers between devices, one_exchange(): tiles = lax.all_to_all(tiles, axis, split_axis=0, concat_axis=0, tiled=True)  52.1 us
    all_to_all x2, starting transfers between devices, one_exchange(): tiles = lax.all_to_all(tiles, axis, split_axis=0, concat_axis=0, tiled=True)  21.7 us
  transfers between devices with their start and end apart: 17, of which 16 were waited for; matrix products, arithmetic and copies ran while one was open for 3% of the time, Pallas kernels for 0%

profile of v1, /device:TPU:1, one launch (start us, length us, event | category | flops | bytes accessed | tf_op | source)
XLA Modules:
  0.0 1038.7 jit_solution(18342659583432440533)
XLA Ops:
  17.6 11.5 %all-to-all-start = ((s32[128,1,2]{2,1,0:T(1,128)}), s32[128,1,2]{2,1,0:T(1,128)S(1)}, u32[]{:S(2)}, u32[]{:S(2)}) async-start(s32[128,1,2]{2,1,0:T(1,128)} %bitcast.16), calls=%async_computation | async-start | bytes 131072 | tf_op jit(solution)/shard_map/all_to_all | solution.py:38
  57.4 10.2 all-to-all-start.1
  68.0 52.1 %all-to-all-done.1 = f32[128,1,2,4096]{3,2,1,0:T(2,128)} async-done(((f32[128,1,2,4096]{3,2,1,0:T(2,128)}), f32[128,1,2,4096]{3,2,1,0:T(2,128)}, u32[]{:S(2)}, u32[]{:S(2)}) %all-to-all-start.1) | async-done | bytes 4194336 | tf_op jit(solution)/shard_map/all_to_all | solution.py:38
  157.4 27.1 %reduce-scatter.3.cloned.1.call-done = f32[72,512]{1,0:T(8,128)} async-done(((f32[576,512]{1,0:T(8,128)}), f32[72,512]{1,0:T(8,128)}) %reduce-scatter.3.cloned.1.call-update) | async-done | bytes 147472 | tf_op jit(solution)/shard_map/reduce_scatter | solution.py:55
  184.5 27.1 %all-gather.3.cloned.1.call-done = f32[576,512]{1,0:T(8,128)} async-done(((f32[72,512]{1,0:T(8,128)}), f32[576,512]{1,0:T(8,128)}) %all-gather.3.cloned.1.call-update) | async-done | bytes 1179664 | tf_op jit(solution)/shard_map/all_gather | solution.py:56
  214.6 23.7 %collective-permute-done = f32[512,512]{1,0:T(8,128)S(1)} collective-permute-done((f32[512,512]{1,0:T(8,128)S(1)}, f32[512,512]{1,0:T(8,128)S(1)}, u32[]{:S(2)}, u32[]{:S(2)}) %collective-permute-start) | collective-permute-done | bytes 1048608 | tf_op jit(solution)/shard_map/ppermute | solution.py:17
  241.5 22.7 %collective-permute-done.1 = f32[512,512]{1,0:T(8,128)S(1)} collective-permute-done((f32[512,512]{1,0:T(8,128)S(1)}, f32[512,512]{1,0:T(8,128)S(1)}, u32[]{:S(2)}, u32[]{:S(2)}) %collective-permute-start.1) | collective-permute-done | bytes 1048608 | tf_op jit(solution)/shard_map/ppermute | solution.py:17
  265.2 22.0 %collective-permute-done.2 = f32[512,512]{1,0:T(8,128)S(1)} collective-permute-done((f32[512,512]{1,0:T(8,128)S(1)}, f32[512,512]{1,0:T(8,128)S(1)}, u32[]{:S(2)}, u32[]{:S(2)}) %collective-permute-start.2) | collective-permute-done | bytes 1048608 | tf_op jit(solution)/shard_map/ppermute | solution.py:17
  290.8 21.5 %collective-permute-done.3 = f32[512,512]{1,0:T(8,128)} collective-permute-done((f32[512,512]{1,0:T(8,128)}, f32[512,512]{1,0:T(8,128)}, u32[]{:S(2)}, u32[]{:S(2)}) %collective-permute-start.3) | collective-permute-done | bytes 1048608 | tf_op jit(solution)/shard_map/ppermute | solution.py:17
  325.7 11.7 %cholesky.286 = f32[128,128]{1,0:T(8,128)S(1)} custom-call(f32[128,128]{1,0:T(8,128)S(1)} %cholesky.426), custom_call_target="Cholesky" | custom-call | tf_op jit(solution)/shard_map/jit(cholesky)/cholesky | solution.py:137
  351.6 11.7 %cholesky.305 = f32[128,128]{1,0:T(8,128)S(1)} custom-call(f32[128,128]{1,0:T(8,128)S(1)} %cholesky.430), custom_call_target="Cholesky" | custom-call | tf_op jit(solution)/shard_map/jit(cholesky)/cholesky | solution.py:137
  363.9 10.2 custom-call.28
  376.5 11.7 %cholesky.326 = f32[128,128]{1,0:T(8,128)S(1)} custom-call(f32[128,128]{1,0:T(8,128)S(1)} %cholesky.435), custom_call_target="Cholesky" | custom-call | tf_op jit(solution)/shard_map/jit(cholesky)/cholesky | solution.py:137
  401.6 11.9 %cholesky.343 = f32[128,128]{1,0:T(8,128)S(1)} custom-call(f32[128,128]{1,0:T(8,128)S(1)} %convolution_subtract_fusion.13), custom_call_target="Cholesky" | custom-call | tf_op jit(solution)/shard_map/jit(cholesky)/cholesky | solution.py:137
  420.4 11.8 %while.4 = (s32[]{:T(128)}, f32[512,512]{1,0:T(8,128)}, s32[4,2]{0,1:T(2,128)S(1)}, f32[4,128,128]{2,1,0:T(8,128)S(1)}, s32[]{:T(128)}) while((s32[]{:T(128)}, f32[512,512]{1,0:T(8,128)}, s32[4,2]{0,1:T(2,128)S(1)}, f32[4,128,128]{2,1,0:T(8,128)S(1)}, s32[]{:T(128)}) %tuple.68), condition=%wide.while_cond, body=%wide.while_body.sunk | while | flops 2 | bytes 131181 | solution.py:138
  432.2 39.3 %custom-call.30 = f32[4,128,128]{1,2,0:T(8,128)S(1)} custom-call(f32[4,128,128]{2,1,0:T(8,128)S(1)} %get-tuple-element.18), custom_call_target="InvertDiagBlocksLowerTriangular" | custom-call | tf_op jit(solution)/shard_map/jit(_solve_triangular)/triangular_solve | solution.py:138
  479.9 93.7 %all-reduce.8.cloned.1.call-done = (f32[576,512]{1,0:T(8,128)}, f32[576,512]{1,0:T(8,128)}) async-done(((f32[576,512]{1,0:T(8,128)}, f32[576,512]{1,0:T(8,128)}), (f32[576,512]{1,0:T(8,128)}, f32[576,512]{1,0:T(8,128)})) %all-reduce.8.cloned.1.call-update) | async-done | bytes 2359312 | tf_op jit(solution)/shard_map/psum | solution.py:61
  584.0 30.4 %reduce-scatter.5.cloned.1.call-done = f32[72,512]{1,0:T(8,128)} async-done(((f32[576,512]{1,0:T(8,128)}), f32[72,512]{1,0:T(8,128)}) %reduce-scatter.5.cloned.1.call-update) | async-done | bytes 147472 | tf_op jit(solution)/shard_map/reduce_scatter | solution.py:55
  614.4 26.9 %all-gather.5.cloned.1.call-done = f32[576,512]{1,0:T(8,128)} async-done(((f32[72,512]{1,0:T(8,128)}), f32[576,512]{1,0:T(8,128)}) %all-gather.5.cloned.1.call-update) | async-done | bytes 1179664 | tf_op jit(solution)/shard_map/all_gather | solution.py:56
  644.7 23.1 %collective-permute-done.4 = f32[512,512]{1,0:T(8,128)S(1)} collective-permute-done((f32[512,512]{1,0:T(8,128)S(1)}, f32[512,512]{1,0:T(8,128)S(1)}, u32[]{:S(2)}, u32[]{:S(2)}) %collective-permute-start.4) | collective-permute-done | bytes 1048608 | tf_op jit(solution)/shard_map/ppermute | solution.py:17
  671.2 22.7 %collective-permute-done.5 = f32[512,512]{1,0:T(8,128)S(1)} collective-permute-done((f32[512,512]{1,0:T(8,128)S(1)}, f32[512,512]{1,0:T(8,128)S(1)}, u32[]{:S(2)}, u32[]{:S(2)}) %collective-permute-start.5) | collective-permute-done | bytes 1048608 | tf_op jit(solution)/shard_map/ppermute | solution.py:17
  694.8 22.1 %collective-permute-done.6 = f32[512,512]{1,0:T(8,128)S(1)} collective-permute-done((f32[512,512]{1,0:T(8,128)S(1)}, f32[512,512]{1,0:T(8,128)S(1)}, u32[]{:S(2)}, u32[]{:S(2)}) %collective-permute-start.6) | collective-permute-done | bytes 1048608 | tf_op jit(solution)/shard_map/ppermute | solution.py:17
  719.8 21.4 %collective-permute-done.7 = f32[512,512]{1,0:T(8,128)} collective-permute-done((f32[512,512]{1,0:T(8,128)S(1)}, f32[512,512]{1,0:T(8,128)}, u32[]{:S(2)}, u32[]{:S(2)}) %collective-permute-start.7) | collective-permute-done | bytes 1048608 | tf_op jit(solution)/shard_map/ppermute | solution.py:17
  749.7 11.7 %cholesky.358 = f32[128,128]{1,0:T(8,128)S(1)} custom-call(f32[128,128]{1,0:T(8,128)S(1)} %cholesky.439), custom_call_target="Cholesky" | custom-call | tf_op jit(solution)/shard_map/jit(cholesky)/cholesky | solution.py:137
  772.1 12.3 %cholesky.377 = f32[128,128]{1,0:T(8,128)} custom-call(f32[128,128]{1,0:T(8,128)S(1)} %cholesky.443), custom_call_target="Cholesky" | custom-call | tf_op jit(solution)/shard_map/jit(cholesky)/cholesky | solution.py:137
  786.8 10.4 %custom-call.32 = f32[1,128,128]{1,2,0:T(8,128)} custom-call(f32[1,128,128]{2,1,0:T(8,128)S(1)} %get-tuple-element.58), custom_call_target="InvertDiagBlocksLowerTriangular" | custom-call | tf_op jit(solution)/shard_map/jit(cholesky)/cholesky | solution.py:137
  798.7 11.7 %cholesky.398 = f32[128,128]{1,0:T(8,128)S(1)} custom-call(f32[128,128]{1,0:T(8,128)S(1)} %cholesky.448), custom_call_target="Cholesky" | custom-call | tf_op jit(solution)/shard_map/jit(cholesky)/cholesky | solution.py:137
  821.5 11.9 %cholesky.415 = f32[128,128]{1,0:T(8,128)S(1)} custom-call(f32[128,128]{1,0:T(8,128)S(1)} %convolution_subtract_fusion.12), custom_call_target="Cholesky" | custom-call | tf_op jit(solution)/shard_map/jit(cholesky)/cholesky | solution.py:137
  845.4 39.3 %custom-call.34 = f32[4,128,128]{1,2,0:T(8,128)S(1)} custom-call(f32[4,128,128]{2,1,0:T(8,128)S(1)} %get-tuple-element.19), custom_call_target="InvertDiagBlocksLowerTriangular" | custom-call | tf_op jit(solution)/shard_map/jit(_solve_triangular)/triangular_solve | solution.py:138
  893.1 93.5 %all-reduce.6.cloned.1.call-done = (f32[576,512]{1,0:T(8,128)}, f32[576,512]{1,0:T(8,128)}) async-done(((f32[576,512]{1,0:T(8,128)}, f32[576,512]{1,0:T(8,128)}), (f32[576,512]{1,0:T(8,128)}, f32[576,512]{1,0:T(8,128)})) %all-reduce.6.cloned.1.call-update) | async-done | bytes 2359312 | tf_op jit(solution)/shard_map/psum | solution.py:61
  993.6 12.7 %fusion.6 = f32[512,576]{1,0:T(8,128)} fusion(f32[576,1152]{1,0:T(8,128)S(1)} %convolution_subtract_fusion, f32[1152,512]{1,0:T(8,128)S(1)} %copy-done.11, pred[1152]{0:T(1024)(128)(4,1)S(1)} %add_compare_fusion), kind=kOutput, calls=%fused_computation.24 | convolution fusion | flops 4077453312 | bytes 6194304 | tf_op jit(solution)/shard_map/dot_general | solution.py:149
  1013.6 17.0 %all-to-all-done.2 = f32[8,64,576]{2,1,0:T(8,128)S(1)} async-done(((f32[8,64,576]{2,1,0:T(8,128)}), f32[8,64,576]{2,1,0:T(8,128)S(1)}, u32[]{:S(2)}, u32[]{:S(2)}) %all-to-all-start.2) | async-done | bytes 1179680 | tf_op jit(solution)/shard_map/all_to_all | solution.py:66
  (201 shorter events, 251.4 us)
Async XLA Ops:
  17.6 39.7 %all-to-all-start = ((s32[128,1,2]{2,1,0:T(1,128)}), s32[128,1,2]{2,1,0:T(1,128)S(1)}, u32[]{:S(2)}, u32[]{:S(2)}) async-start(s32[128,1,2]{2,1,0:T(1,128)} %bitcast.16), calls=%async_computation | async-start | bytes 131072 | tf_op jit(solution)/shard_map/all_to_all | solution.py:38
  57.4 62.7 %all-to-all-start.1 = ((f32[128,1,2,4096]{3,2,1,0:T(2,128)}), f32[128,1,2,4096]{3,2,1,0:T(2,128)}, u32[]{:S(2)}, u32[]{:S(2)}) async-start(f32[128,1,2,4096]{3,2,1,0:T(2,128)} %bitcast.188), calls=%async_computation.1 | async-start | bytes 8388608 | tf_op jit(solution)/shard_map/all_to_all | solution.py:38
  67.6 116.9 %reduce-scatter.3.cloned.1.call-start = ((), (), s32[]{:S(2)}) async-start(), calls=%async_computation.5 | async-start | bytes 1327104 | tf_op jit(solution)/shard_map/reduce_scatter | solution.py:55
  154.6 1.5 copy-start
  157.3 54.3 %all-gather.3.cloned.1.call-start = ((), (), s32[]{:S(2)}) async-start(), calls=%async_computation.6 | async-start | bytes 1327104 | tf_op jit(solution)/shard_map/all_gather | solution.py:56
  184.5 389.1 %all-reduce.8.cloned.1.call-start = ((), (), s32[]{:S(2)}) async-start(), calls=%async_computation.10 | async-start | bytes 4718592 | tf_op jit(solution)/shard_map/psum | solution.py:61
  211.7 26.6 %copy-start.3 = (f32[576,512]{1,0:T(8,128)S(1)}, f32[576,512]{1,0:T(8,128)}, u32[]{:S(2)}) copy-start(f32[576,512]{1,0:T(8,128)} %all-gather.3.cloned.1.call-done) | copy-start | bytes 3538948
  213.8 24.5 %collective-permute-start = (f32[512,512]{1,0:T(8,128)S(1)}, f32[512,512]{1,0:T(8,128)S(1)}, u32[]{:S(2)}, u32[]{:S(2)}) collective-permute-start(f32[512,512]{1,0:T(8,128)S(1)} %fusion.17), channel_id=1, source_target_pairs={{0,8},{8,0},{16,24},{24,16},{32,40},{40,32},{48,56},{56,48},{64,72... | collective-permute-start | bytes 3145736 | tf_op jit(solution)/shard_map/ppermute | solution.py:17
  239.1 25.2 %collective-permute-start.1 = (f32[512,512]{1,0:T(8,128)S(1)}, f32[512,512]{1,0:T(8,128)S(1)}, u32[]{:S(2)}, u32[]{:S(2)}) collective-permute-start(f32[512,512]{1,0:T(8,128)S(1)} %fusion.130), channel_id=1, source_target_pairs={{0,16},{8,24},{16,0},{24,8},{32,48},{40,56},{48,32},{56,40},{64,80... | collective-permute-start | bytes 3145736 | tf_op jit(solution)/shard_map/ppermute | solution.py:17
  264.5 22.8 %collective-permute-start.2 = (f32[512,512]{1,0:T(8,128)S(1)}, f32[512,512]{1,0:T(8,128)S(1)}, u32[]{:S(2)}, u32[]{:S(2)}) collective-permute-start(f32[512,512]{1,0:T(8,128)S(1)} %add.271), channel_id=1, source_target_pairs={{0,32},{8,40},{16,48},{24,56},{32,0},{40,8},{48,16},{56,24},{64,96... | collective-permute-start | bytes 3145736 | tf_op jit(solution)/shard_map/ppermute | solution.py:17
  288.5 23.8 %collective-permute-start.3 = (f32[512,512]{1,0:T(8,128)}, f32[512,512]{1,0:T(8,128)}, u32[]{:S(2)}, u32[]{:S(2)}) collective-permute-start(f32[512,512]{1,0:T(8,128)} %add.272), channel_id=1, source_target_pairs={{0,64},{8,72},{16,80},{24,88},{32,96},{40,104},{48,112},{56,120},{... | collective-permute-start | bytes 3145736 | tf_op jit(solution)/shard_map/ppermute | solution.py:17
  324.7 1.0 copy-start.9
  479.9 134.5 %reduce-scatter.5.cloned.1.call-start = ((), (), s32[]{:S(2)}) async-start(), calls=%async_computation.7 | async-start | bytes 1327104 | tf_op jit(solution)/shard_map/reduce_scatter | solution.py:55
  581.2 1.5 copy-start.1
  583.9 57.4 %all-gather.5.cloned.1.call-start = ((), (), s32[]{:S(2)}) async-start(), calls=%async_computation.8 | async-start | bytes 1327104 | tf_op jit(solution)/shard_map/all_gather | solution.py:56
  614.4 372.2 %all-reduce.6.cloned.1.call-start = ((), (), s32[]{:S(2)}) async-start(), calls=%async_computation.9 | async-start | bytes 4718592 | tf_op jit(solution)/shard_map/psum | solution.py:61
  641.4 26.4 %copy-start.4 = (f32[576,512]{1,0:T(8,128)S(1)}, f32[576,512]{1,0:T(8,128)}, u32[]{:S(2)}) copy-start(f32[576,512]{1,0:T(8,128)} %all-gather.5.cloned.1.call-done) | copy-start | bytes 3538948
  643.1 24.7 %collective-permute-start.4 = (f32[512,512]{1,0:T(8,128)S(1)}, f32[512,512]{1,0:T(8,128)S(1)}, u32[]{:S(2)}, u32[]{:S(2)}) collective-permute-start(f32[512,512]{1,0:T(8,128)S(1)} %fusion.15), channel_id=1, source_target_pairs={{0,8},{8,0},{16,24},{24,16},{32,40},{40,32},{48,56},{56,48},{64,72... | collective-permute-start | bytes 3145736 | tf_op jit(solution)/shard_map/ppermute | solution.py:17
  668.6 25.3 %collective-permute-start.5 = (f32[512,512]{1,0:T(8,128)S(1)}, f32[512,512]{1,0:T(8,128)S(1)}, u32[]{:S(2)}, u32[]{:S(2)}) collective-permute-start(f32[512,512]{1,0:T(8,128)S(1)} %fusion.129), channel_id=1, source_target_pairs={{0,16},{8,24},{16,0},{24,8},{32,48},{40,56},{48,32},{56,40},{64,80... | collective-permute-start | bytes 3145736 | tf_op jit(solution)/shard_map/ppermute | solution.py:17
  694.0 22.9 %collective-permute-start.6 = (f32[512,512]{1,0:T(8,128)S(1)}, f32[512,512]{1,0:T(8,128)S(1)}, u32[]{:S(2)}, u32[]{:S(2)}) collective-permute-start(f32[512,512]{1,0:T(8,128)S(1)} %add.278), channel_id=1, source_target_pairs={{0,32},{8,40},{16,48},{24,56},{32,0},{40,8},{48,16},{56,24},{64,96... | collective-permute-start | bytes 3145736 | tf_op jit(solution)/shard_map/ppermute | solution.py:17
  717.2 24.1 %collective-permute-start.7 = (f32[512,512]{1,0:T(8,128)S(1)}, f32[512,512]{1,0:T(8,128)}, u32[]{:S(2)}, u32[]{:S(2)}) collective-permute-start(f32[512,512]{1,0:T(8,128)S(1)} %add.279), channel_id=1, source_target_pairs={{0,64},{8,72},{16,80},{24,88},{32,96},{40,104},{48,112},{56,120},{... | collective-permute-start | bytes 3145736 | tf_op jit(solution)/shard_map/ppermute | solution.py:17
  748.7 1.0 copy-start.7
  749.7 21.7 %copy-start.8 = (f32[512,512]{1,0:T(8,128)S(1)}, f32[512,512]{1,0:T(8,128)}, u32[]{:S(2)}) copy-start(f32[512,512]{1,0:T(8,128)} %copy-done.7) | copy-start | bytes 3145732
  845.4 39.3 %copy-start.6 = (f32[512,512]{1,0:T(8,128)}, f32[512,512]{1,0:T(8,128)S(1)}, u32[]{:S(2)}) copy-start(f32[512,512]{1,0:T(8,128)S(1)} %get-tuple-element.213) | copy-start | bytes 3145732
  890.9 2.1 copy-start.10
  890.9 95.7 %copy-start.2 = (f32[576,1152]{1,0:T(8,128)S(1)}, f32[576,1152]{1,0:T(8,128)}, u32[]{:S(2)}) copy-start(f32[576,1152]{1,0:T(8,128)} %copy-done.1) | copy-start | bytes 7962628
  986.6 7.0 copy-start.11
  1006.3 6.5 copy-start.5
  1006.3 24.3 %all-to-all-start.2 = ((f32[8,64,576]{2,1,0:T(8,128)}), f32[8,64,576]{2,1,0:T(8,128)S(1)}, u32[]{:S(2)}, u32[]{:S(2)}) async-start(f32[8,64,576]{2,1,0:T(8,128)} %bitcast.63), calls=%async_computation.4 | async-start | bytes 2621440 | tf_op jit(solution)/shard_map/all_to_all | solution.py:66
Sparse Core Ops, SparseCore 0:
  157.5 26.9 reduce-scatter.2
  186.1 25.4 all-gather.2
  480.0 93.5 all-reduce.7
  584.1 30.2 reduce-scatter.4
  615.9 25.4 all-gather.4
  893.2 93.3 all-reduce.5
